TPU v7x, 512 devices: a whole 4x4x16 slice. The times are simulated.
512 devices in a mesh: row: 16 (over z), col: 8 (over x, core), depth: 4 (over y).
Axes of the slice: x: 4, y: 4, z: 16, core: 2. Of those that a mesh axis runs over, the one named last changes fastest.
Arguments:
- eri_tiles: bfloat16 [192, 256, 128, 128], P('row', ('col', 'depth')), may hold values from -0.03125 to 0.03125
- screen: int32 [192, 256], P('row', ('col', 'depth')), may hold values from 0 to 1, as said below
- density_bra: bfloat16 [24576, 256], P('row', 'col'), may hold values from -6 to 6
- density_ket: bfloat16 [32768, 256], P(('col', 'depth'), 'row'), may hold values from -6 to 6
Outputs:
- coulomb_bra: float32 [24576, 256], P('row', 'col')
- coulomb_ket: float32 [32768, 256], P(('col', 'depth'), 'row')
Inputs may be any that keep to these rules, and one draw needn't show every extreme that they name: `screen`: in each device's block of 12 x 8 tiles (aligned blocks), between 16 and 64 tiles are significant; some block has exactly 64.
All inputs are finite; a program needn't handle non-finite values.
Results may differ from a plain program's by a relative error of at most 0.005.
Values may be sent and summed in bfloat16 or wider, within the bound.
A program may use at most 64 MiB of HBM per device.

v0:
```python
import jax
import jax.numpy as jnp
from jax import lax
from jax.sharding import PartitionSpec as P


def from_everyone(array, axis):
    copies = jnp.broadcast_to(array, (lax.axis_size(axis), *array.shape))
    return lax.all_to_all(copies, axis, split_axis=0, concat_axis=0, tiled=True)


def joined_along(pieces, dim):
    pieces = jnp.moveaxis(pieces, 0, dim)
    shape = pieces.shape
    return pieces.reshape(*shape[:dim], shape[dim] * shape[dim + 1], *shape[dim + 2 :])


def gather_directly(array, axis, dim):
    pieces = from_everyone(array, axis)
    return joined_along(pieces, dim)


def split_up(array, dim, length):
    before, after = (array.shape[:dim], array.shape[dim + 1 :])
    return jnp.moveaxis(array.reshape(*before, length, -1, *after), dim, 0)


def sum_at_owner(array, axis, dim):
    length = lax.axis_size(axis)
    pieces = lax.all_to_all(split_up(array, dim, length), axis, 0, 0, tiled=True)
    return jnp.sum(pieces, axis=0)


def body(eri_tiles, screen, density_bra, density_ket):
    blocks_a = eri_tiles.shape[0]
    blocks_b = eri_tiles.shape[1]
    pair_size = eri_tiles.shape[2]
    masked = jnp.where(screen[:, :, None, None] > 0, eri_tiles, jnp.zeros((), jnp.bfloat16))
    fragment = gather_directly(density_ket, "row", 1)
    columns = fragment.shape[1]
    shaped = fragment.reshape(blocks_b, pair_size, columns)
    summed = jnp.einsum("abij,bjc->aic", masked, shaped, preferred_element_type=jnp.float32)
    bra_part = summed.reshape(blocks_a * pair_size, columns)
    fragment = gather_directly(density_bra, "col", 1)
    columns = fragment.shape[1]
    shaped = fragment.reshape(blocks_a, pair_size, columns)
    summed = jnp.einsum("abij,aic->bjc", masked, shaped, preferred_element_type=jnp.float32)
    ket_part = summed.reshape(blocks_b * pair_size, columns)
    coulomb_ket = lax.psum_scatter(ket_part, "row", scatter_dimension=1, tiled=True)
    shares = sum_at_owner(bra_part, ("col", "depth"), 1)
    coulomb_bra = gather_directly(shares, "depth", 1)
    return (coulomb_bra, coulomb_ket)


def solution(mesh):
    return jax.shard_map(
        body,
        mesh=mesh,
        in_specs=(
            P("row", ("col", "depth"), None, None),
            P("row", ("col", "depth")),
            P("row", "col"),
            P(("col", "depth"), "row"),
        ),
        out_specs=(P("row", "col"), P(("col", "depth"), "row")),
        check_vma=False,
    )
```

profile of v0, /device:TPU:8, one launch (start us, length us, event | category | flops | bytes accessed | tf_op | source)
XLA Modules:
  0.0 140.1 jit_solution(16489293856440860099)
XLA Ops:
  7.2 0.0 copy-start.2
  7.2 0.0 copy-start
  7.2 1.1 broadcast_in_dim.26
  8.3 17.4 %all_to_all.20 = bf16[8,1536,32]{1,2,0:T(8,128)(2,1)} all-to-all(bf16[8,1536,32]{1,2,0:T(8,128)(2,1)S(1)} %broadcast_in_dim.26), channel_id=1, replica_groups=mesh['row'=16,'col'=8,'depth'=4] {'col'}, dimensions={0} | all-to-all | bytes 1572864 | tf_op jit(solution)/shard_map/all_to_all | solution.py:9
  25.7 1.7 %broadcast_in_dim.24 = bf16[16,1024,16]{1,2,0:T(8,128)(2,1)} broadcast(bf16[1024,16]{0,1:T(8,128)(2,1)} %param.7), dimensions={1,2} | broadcast | bytes 557056 | tf_op jit(solution)/shard_map/broadcast_in_dim | solution.py:8
  27.3 15.2 %all-to-all-start = ((bf16[16,1024,16]{1,2,0:T(8,128)(2,1)}), bf16[16,1024,16]{1,2,0:T(8,128)(2,1)}, u32[]{:S(2)}, u32[]{:S(2)}) async-start(bf16[16,1024,16]{1,2,0:T(8,128)(2,1)} %broadcast_in_dim.24), calls=%async_computation | async-start | bytes 1048576 | tf_op jit(solution)/shard_map/all_to_all | solution.py:9
  42.6 0.0 reduce-scatter.2.cloned.1.call-start
  42.6 0.0 copy-done.2
  42.7 0.1 copy.15
  42.8 0.0 copy-done
  42.8 3.7 %fusion.9 = bf16[8,128,12,128]{1,0,3,2:T(8,128)(2,1)} fusion(bf16[12,8,128,128]{3,2,1,0:T(8,128)(2,1)S(1)} %copy-done, pred[12,8]{1,0:T(8,128)(4,1)S(1)} %copy.15), kind=kLoop, calls=%fused_computation.9 | loop fusion | flops 1572864 | bytes 6291552 | tf_op jit(solution)/shard_map/abij,aic->bjc/dot_general | solution.py:47
  46.4 4.9 %copy.20 = bf16[8,128,12,128]{3,1,0,2:T(8,128)(2,1)} copy(bf16[8,128,12,128]{1,0,3,2:T(8,128)(2,1)} %fusion.9) | data formatting | bytes 6291456 | tf_op jit(solution)/shard_map/abij,aic->bjc/dot_general | solution.py:47
  51.4 3.7 %copy_select_fusion = bf16[12,8,128,128]{3,1,2,0:T(8,128)(2,1)} fusion(bf16[12,8,128,128]{3,2,1,0:T(8,128)(2,1)S(1)} %copy-done, pred[12,8]{1,0:T(8,128)(4,1)S(1)} %copy.15), kind=kLoop, calls=%fused_computation.3 | loop fusion | flops 1572864 | bytes 6291552 | tf_op jit(solution)/shard_map/jit(_where)/select_n | solution.py:38
  55.0 2.4 %reshape_reshape.8 = bf16[12,128,256]{1,0,2:T(8,128)(2,1)} reshape(bf16[1536,8,32]{0,2,1:T(8,128)(2,1)} %bitcast.35) | data formatting | bytes 1572864 | tf_op jit(solution)/shard_map/reshape;reshape | solution.py:46
  57.4 0.0 copy-start.1
  57.4 4.3 %convolution_bitcast_fusion = f32[1024,256]{0,1:T(8,128)} fusion(bf16[1024,12,128]{2,0,1:T(8,128)(2,1)} %bitcast.37, bf16[12,128,256]{1,0,2:T(8,128)(2,1)} %reshape_reshape.8), kind=kOutput, calls=%fused_computation.5 | convolution fusion | flops 805306368 | bytes 4980736 | tf_op jit(solution)/shard_map/abij,aic->bjc/dot_general | solution.py:47
  61.8 0.0 reduce-scatter.2.cloned.1.call-update
  61.8 9.4 %all-to-all-done = bf16[16,1024,16]{1,2,0:T(8,128)(2,1)} async-done(((bf16[16,1024,16]{1,2,0:T(8,128)(2,1)}), bf16[16,1024,16]{1,2,0:T(8,128)(2,1)}, u32[]{:S(2)}, u32[]{:S(2)}) %all-to-all-start) | async-done | bytes 524320 | tf_op jit(solution)/shard_map/all_to_all | solution.py:9
  71.2 1.1 copy.23
  72.3 0.0 copy-done.1
  72.4 1.1 fusion.3
  73.5 0.9 copy.19
  74.4 26.4 %all_to_all.21 = f32[32,1536,8]{1,2,0:T(8,128)S(1)} all-to-all(f32[32,1536,8]{1,2,0:T(8,128)S(1)} %copy.19), channel_id=1, replica_groups=mesh['row'=16,'col'=8,'depth'=4] {'col','depth'}, dimensions={0} | all-to-all | bytes 3145728 | tf_op jit(solution)/shard_map/all_to_all | solution.py:30
  100.8 0.1 reduce_sum.9
  100.9 9.6 %all_to_all.22 = f32[4,1536,8]{1,2,0:T(8,128)S(1)} all-to-all(f32[4,1536,8]{1,2,0:T(8,128)S(1)} %broadcast_in_dim.25), channel_id=1, replica_groups=mesh['row'=16,'col'=8,'depth'=4] {'depth'}, dimensions={0} | all-to-all | bytes 393216 | tf_op jit(solution)/shard_map/all_to_all | solution.py:9
  110.5 22.1 %reduce-scatter.2.cloned.1.call-done = f32[1024,16]{0,1:T(8,128)} async-done(((f32[1024,256]{0,1:T(8,128)}), f32[1024,16]{0,1:T(8,128)}) %reduce-scatter.2.cloned.1.call-update) | async-done | bytes 65552 | tf_op jit(solution)/shard_map/reduce_scatter | solution.py:49
  132.6 0.7 copy.38
  (2 shorter events, 0.0 us)
Async XLA Ops:
  7.2 35.5 %copy-start.2 = (s32[12,8]{0,1:T(8,128)S(1)}, s32[12,8]{0,1:T(8,128)}, u32[]{:S(2)}) copy-start(s32[12,8]{0,1:T(8,128)} %param.5) | copy-start | bytes 1156
  7.2 35.6 %copy-start = (bf16[12,8,128,128]{3,2,1,0:T(8,128)(2,1)S(1)}, bf16[12,8,128,128]{3,2,1,0:T(8,128)(2,1)}, u32[]{:S(2)}) copy-start(bf16[12,8,128,128]{3,2,1,0:T(8,128)(2,1)} %param.4) | copy-start | bytes 9437188
  27.3 43.9 %all-to-all-start = ((bf16[16,1024,16]{1,2,0:T(8,128)(2,1)}), bf16[16,1024,16]{1,2,0:T(8,128)(2,1)}, u32[]{:S(2)}, u32[]{:S(2)}) async-start(bf16[16,1024,16]{1,2,0:T(8,128)(2,1)} %broadcast_in_dim.24), calls=%async_computation | async-start | bytes 1048576 | tf_op jit(solution)/shard_map/all_to_all | solution.py:9
  42.6 90.0 %reduce-scatter.2.cloned.1.call-start = ((), (), s32[]{:S(2)}) async-start(), calls=%async_computation.5 | async-start | bytes 1114112 | tf_op jit(solution)/shard_map/reduce_scatter | solution.py:49
  57.4 14.9 %copy-start.1 = (bf16[12,8,128,128]{3,1,2,0:T(8,128)(2,1)S(1)}, bf16[12,8,128,128]{3,1,2,0:T(8,128)(2,1)}, u32[]{:S(2)}) copy-start(bf16[12,8,128,128]{3,1,2,0:T(8,128)(2,1)} %copy_select_fusion) | copy-start | bytes 9437188
Sparse Core Ops, SparseCore 0:
  61.9 70.6 reduce-scatter.1
where the time goes:
time: 141 us; the launch traced here: 140 us
  blocking collectives  53.4 us (38%)
  waiting for transfers between devices  31.6 us (22%)
  starting transfers between devices  15.3 us (11%)
  between operations  14.1 us (10%)
  local copies, waits for them, and re-layouts  12.9 us (9%)
  other arithmetic  7.44 us (5%)
  matrix products  5.44 us (4%)
    all_to_all x2, blocking collectives, from_everyone(): return lax.all_to_all(copies, axis, split_axis=0, concat_axis=0, tiled=True)  27 us
    all_to_all x1, blocking collectives, sum_at_owner(): lax.all_to_all(split_up(array, dim, length), axis, 0, 0, tiled=True)  26.4 us
    reduce_scatter x1, waiting for transfers between devices, body(): lax.psum_scatter(ket_part, 'row', scatter_dimension=1, tiled=True)  22.1 us
    all_to_all x1, starting transfers between devices, from_everyone(): return lax.all_to_all(copies, axis, split_axis=0, concat_axis=0, tiled=True)  15.2 us
    all_to_all x1, waiting for transfers between devices, from_everyone(): return lax.all_to_all(copies, axis, split_axis=0, concat_axis=0, tiled=True)  9.42 us
    dot_general x1, local copies, waits for them, and re-layouts, body(): jnp.einsum('abij,aic->bjc', masked, shaped, preferred_element_type=jnp.fl...  4.93 us
    dot_general x1, matrix products, body(): jnp.einsum('abij,aic->bjc', masked, shaped, preferred_element_type=jnp.fl...  4.33 us
    dot_general x1, other arithmetic, body(): jnp.einsum('abij,aic->bjc', masked, shaped, preferred_element_type=jnp.fl...  3.67 us
  transfers between devices with their start and end apart: 2, of which 2 were waited for; matrix products, arithmetic and copies ran while one was open for 16% of the time, Pallas kernels for 0%

commit v1 on v0

v1 whole, which is shorter than its diff:
```python
import jax
import jax.numpy as jnp
from jax import lax
from jax.experimental import pallas as pl
from jax.experimental.pallas import tpu as pltpu
from jax.sharding import PartitionSpec as P

MESH = pl.DeviceIdType.MESH
F32 = jnp.float32
BF16 = jnp.bfloat16

NZ, NX, NY = 16, 4, 4
NA_DEV, NB_DEV, PAIR = 12, 8, 128
ROWS_A, ROWS_B = NA_DEV * PAIR, NB_DEV * PAIR
HALF_A, HALF_B = ROWS_A // 2, ROWS_B // 2
STRIP = 16

PARENT = {}
for sign in (1, -1):
    for dist in (1, 2):
        PARENT[sign * dist] = 0
    for dist in range(3, 9):
        PARENT[sign * dist] = sign * (2 * ((dist - 1) // 2))
LEVELS = ((1, -1, 2, -2), (3, -3, 4, -4), (5, -5, 6, -6), (7, -7, 8, -8))
GROUPS = ((0, 1, -1, 2, -2), (3, -3, 4, -4), (5, -5, 6, -6), (7, -7, 8))


def kernel(
    eri_hbm, screen_ref, bra_hbm, ket_hbm,
    out_bra, out_ket,
    tiles, matrix, dbra, dket, ket_acc, rs_recv, rs_send,
    bra_part, bra_recv, bra_red, x_recv, y_sum, y_recv, f_sum, f_recv,
    load_sem, tile_sem,
    ag_send, ag_recv, x_send, x_rsem, d_send, d_recv,
    rs_ssem, rs_rsem, c_send, c_recv, xr_send, xr_recv, y_send, y_rsem, f_send, f_rsem,
):
    z = lax.axis_index("row")
    col = lax.axis_index("col")
    y = lax.axis_index("depth")
    x = col // 2
    core = lax.rem(col, 2)
    other = 1 - core

    def z_at(offset):
        return lax.rem(z + offset + 2 * NZ, NZ)

    def x_at(offset):
        return lax.rem(x + offset, NX)

    def y_at(offset):
        return lax.rem(y + offset, NY)

    def remote(src, dst, ssem, rsem, **where):
        return pltpu.make_async_remote_copy(
            src_ref=src, dst_ref=dst, send_sem=ssem, recv_sem=rsem,
            device_id=where, device_id_type=MESH,
        )

    loads = [pltpu.make_async_copy(bra_hbm, dbra.at[col], load_sem.at[0])]
    for h in range(2):
        loads.append(
            pltpu.make_async_copy(
                ket_hbm.at[:, pl.ds(h * HALF_B, HALF_B)], dket.at[z, h], load_sem.at[1 + h]
            )
        )
    for copy in loads:
        copy.start()
    tile_loads = [
        pltpu.make_async_copy(eri_hbm.at[a], tiles.at[a], tile_sem.at[a]) for a in range(NA_DEV)
    ]
    for copy in tile_loads:
        copy.start()

    barrier = pltpu.get_barrier_semaphore()
    peers = []
    for step in (1, -1, 2, -2):
        peers.append({"row": z_at(step)})
    for offset in range(1, NX):
        peers.append({"col": 2 * x_at(offset) + core})
    peers.append({"col": 2 * x + other})
    for offset in range(1, NY):
        peers.append({"depth": y_at(offset), "col": 2 * x})
        peers.append({"depth": y_at(offset), "col": 2 * x + 1})
    for peer in peers:
        pl.semaphore_signal(barrier, inc=1, device_id=peer, device_id_type=MESH)
    pl.semaphore_wait(barrier, len(peers))

    for copy in loads:
        copy.wait()

    sends = []
    for offset in (2, 1, 3):
        copy = remote(
            dbra.at[col], dbra.at[col], x_send.at[offset - 1], x_rsem.at[offset - 1],
            col=2 * x_at(offset) + core,
        )
        copy.start()
        sends.append(copy)
    copy = remote(dbra.at[col], dbra.at[col], d_send.at[0], d_recv.at[0], col=2 * x + other)
    copy.start()
    sends.append(copy)

    def ag_copy(offset):
        parent = PARENT[offset]
        slot = z_at(-parent)
        if abs(offset) == 8:
            h = 0 if offset > 0 else 1
            src, dst = dket.at[slot, h], dket.at[slot, h]
        else:
            src, dst = dket.at[slot], dket.at[slot]
        index = offset + 8
        return remote(src, dst, ag_send.at[index], ag_recv.at[index], row=z_at(offset - parent))

    def ag_wait(offset):
        slot = z_at(-offset)
        if abs(offset) == 8:
            ref = dket.at[slot, 0 if offset > 0 else 1]
        else:
            ref = dket.at[slot]
        index = offset + 8
        remote(ref, ref, ag_send.at[index], ag_recv.at[index], row=z_at(1)).wait_recv()

    def ag_forward(offset):
        for child, parent in PARENT.items():
            if parent == offset:
                copy = ag_copy(child)
                copy.start()
                sends.append(copy)

    ag_forward(0)

    for a in range(NA_DEV):
        tile_loads[a].wait()
        for b in range(NB_DEV):
            keep = screen_ref[b, a] > 0
            matrix[a * PAIR : (a + 1) * PAIR, b * PAIR : (b + 1) * PAIR] = jnp.where(
                keep, tiles[a, b], jnp.zeros((PAIR, PAIR), BF16)
            )

    def ket_group(xs):
        rows = jnp.concatenate([dbra[2 * xx + i] for xx in xs for i in range(2)], axis=0)
        for n in range(4):
            part = jnp.dot(
                rows, matrix[:, n * 256 : (n + 1) * 256], preferred_element_type=F32
            )
            for g, xx in enumerate(xs):
                for q in range(4):
                    lo = (4 * g + q) * STRIP
                    ket_acc[4 * xx + q, n // 2, :, (n % 2) * 256 : (n % 2 + 1) * 256] = part[
                        lo : lo + STRIP
                    ]

    def ag_level(level):
        for offset in LEVELS[level]:
            ag_wait(offset)
            ag_forward(offset)

    def d_copy(index, column):
        return remote(
            dbra.at[column], dbra.at[column], d_send.at[index], d_recv.at[index], col=2 * x + other
        )

    d_copy(0, 2 * x + other).wait_recv()
    ket_group([x])
    ag_level(0)
    for offset in (1, 3, 2):
        source = 2 * x_at(NX - offset)
        remote(
            dbra.at[source + core], dbra.at[source + core],
            x_send.at[offset - 1], x_rsem.at[offset - 1], col=2 * x + other,
        ).wait_recv()
        copy = d_copy(offset, source + core)
        copy.start()
        sends.append(copy)
    ag_level(1)
    for offset in (1, 3, 2):
        d_copy(offset, 2 * x_at(NX - offset) + other).wait_recv()
    ket_group([x_at(3), x_at(1), x_at(2)])

    def rs_copy(way, step, h, src):
        sign = 1 - 2 * way
        return remote(
            src, rs_recv.at[way, step - 1, h],
            rs_ssem.at[way, step - 1, h], rs_rsem.at[way, step - 1, h], row=z_at(sign),
        )

    def rs_exists(way, step, h):
        return step >= 2 or h == way

    def rs_step(step):
        for h in range(2):
            for way in range(2):
                if not rs_exists(way, step, h):
                    continue
                target = z_at((1 - 2 * way) * (9 - step))
                if step >= 2 and rs_exists(way, step - 1, h):
                    rs_copy(way, step - 1, h, rs_recv.at[way, step - 2, h]).wait_recv()
                    rs_send[way, step - 1, h] = ket_acc[target, h] + rs_recv[way, step - 2, h]
                    src = rs_send.at[way, step - 1, h]
                else:
                    src = ket_acc.at[target, h]
                copy = rs_copy(way, step, h, src)
                copy.start()
                sends.append(copy)

    def c_copy(offset, slot, h):
        return remote(
            bra_part.at[slot, h], bra_recv.at[slot],
            c_send.at[offset + 7], c_recv.at[offset + 7], col=2 * x + other,
        )

    def bra_group(group):
        slots = [z_at(-offset) for offset in group]
        rows = jnp.concatenate(
            [jnp.concatenate([dket[slot, 0], dket[slot, 1]], axis=1) for slot in slots], axis=0
        )
        for n in range(6):
            part = lax.dot_general(
                rows, matrix[n * 256 : (n + 1) * 256, :],
                (((1,), (1,)), ((), ())), preferred_element_type=F32,
            )
            for i, slot in enumerate(slots):
                bra_part[slot, n // 3, :, (n % 3) * 256 : (n % 3 + 1) * 256] = part[
                    i * STRIP : (i + 1) * STRIP
                ]
        for offset, slot in zip(group, slots):
            copy = c_copy(offset, slot, other)
            copy.start()
            sends.append(copy)

    def xr_copy(offset, slot):
        target = slot // 4
        away = lax.rem(target - x + NX, NX)
        index = lax.max(away - 1, 0)
        return away, remote(
            bra_red.at[slot], x_recv.at[index, lax.rem(slot, 4)],
            xr_send.at[offset + 7], xr_recv.at[index, lax.rem(slot, 4)],
            col=2 * target + core,
        )

    def bra_reduce(group):
        for offset in group:
            slot = z_at(-offset)
            c_copy(offset, slot, core).wait_recv()
            bra_red[slot] = bra_part[slot, core] + bra_recv[slot]
            away, copy = xr_copy(offset, slot)

            @pl.when(away != 0)
            def _():
                copy.start()

    rs_step(1)
    bra_group(GROUPS[0])
    ag_level(2)
    rs_step(2)
    bra_reduce(GROUPS[0])
    bra_group(GROUPS[1])
    rs_step(3)
    ag_level(3)
    bra_reduce(GROUPS[1])
    bra_group(GROUPS[2])
    rs_step(4)
    bra_reduce(GROUPS[2])
    bra_group(GROUPS[3])
    rs_step(5)
    bra_reduce(GROUPS[3])

    def y_copy(offset):
        target = y_at(offset)
        return remote(
            y_sum.at[target], y_recv.at[offset - 1], y_send.at[offset - 1], y_rsem.at[offset - 1],
            depth=target,
        )

    rs_step(6)
    for q in range(4):
        total = bra_red[4 * x + q]
        for index in range(3):
            remote(
                bra_red.at[4 * x + q], x_recv.at[index, q], xr_send.at[0], xr_recv.at[index, q],
                col=2 * x_at(1) + core,
            ).wait_recv()
            total = total + x_recv[index, q]
        y_sum[q] = total
    for offset in (2, 1, 3):
        copy = y_copy(offset)
        copy.start()
        sends.append(copy)
    rs_step(7)
    rs_step(8)
    total = y_sum[y]
    for offset in (1, 3, 2):
        y_copy(offset).wait_recv()
        total = total + y_recv[offset - 1]
    f_sum[...] = total
    owner = y // 2
    piece = 2 * lax.rem(y, 2) + core

    def f_copy(offset):
        return remote(
            f_sum, f_recv.at[piece], f_send.at[offset], f_rsem.at[piece],
            depth=y_at(offset), col=2 * x + owner,
        )

    for offset in (2, 1, 3):
        copy = f_copy(offset)
        copy.start()
        sends.append(copy)

    @pl.when(owner != core)
    def _():
        f_copy(0).start()

    @pl.when(owner == core)
    def _():
        f_recv[piece] = total

    for h in range(2):
        total = ket_acc[z, h]
        for way in range(2):
            rs_copy(way, 8, h, rs_recv.at[way, 7, h]).wait_recv()
            total = total + rs_recv[way, 7, h]
        out_ket[:, h * HALF_B : (h + 1) * HALF_B] = total

    for p in range(4):
        mine = jnp.logical_and(owner == core, piece == p)

        @pl.when(jnp.logical_not(mine))
        def _():
            remote(f_sum, f_recv.at[p], f_send.at[0], f_rsem.at[p], depth=y_at(1), col=col).wait_recv()

        out_bra[
            (p // 2) * STRIP : (p // 2 + 1) * STRIP, (p % 2) * HALF_A : (p % 2 + 1) * HALF_A
        ] = f_recv[p]

    for copy in sends:
        copy.wait_send()
    for group in GROUPS:
        for offset in group:
            away, copy = xr_copy(offset, z_at(-offset))

            @pl.when(away != 0)
            def _():
                copy.wait_send()

    @pl.when(owner != core)
    def _():
        f_copy(0).wait_send()


def body(eri_tiles, screen, density_bra, density_ket):
    any_spec = pl.BlockSpec(memory_space=pl.ANY)
    vmem_spec = pl.BlockSpec(memory_space=pltpu.VMEM)
    dma = pltpu.SemaphoreType.DMA
    bra_t, ket_t = pl.pallas_call(
        kernel,
        out_shape=(
            jax.ShapeDtypeStruct((32, ROWS_A), F32),
            jax.ShapeDtypeStruct((STRIP, ROWS_B), F32),
        ),
        in_specs=[any_spec, pl.BlockSpec(memory_space=pltpu.SMEM), any_spec, any_spec],
        out_specs=(vmem_spec, vmem_spec),
        scratch_shapes=[
            pltpu.VMEM((NA_DEV, NB_DEV, PAIR, PAIR), BF16),
            pltpu.VMEM((ROWS_A, ROWS_B), BF16),
            pltpu.VMEM((8, 32, ROWS_A), BF16),
            pltpu.VMEM((NZ, 2, STRIP, HALF_B), BF16),
            pltpu.VMEM((NZ, 2, STRIP, HALF_B), F32),
            pltpu.VMEM((2, 8, 2, STRIP, HALF_B), F32),
            pltpu.VMEM((2, 8, 2, STRIP, HALF_B), F32),
            pltpu.VMEM((NZ, 2, STRIP, HALF_A), F32),
            pltpu.VMEM((NZ, STRIP, HALF_A), F32),
            pltpu.VMEM((NZ, STRIP, HALF_A), F32),
            pltpu.VMEM((3, 4, STRIP, HALF_A), F32),
            pltpu.VMEM((4, STRIP, HALF_A), F32),
            pltpu.VMEM((3, STRIP, HALF_A), F32),
            pltpu.VMEM((STRIP, HALF_A), F32),
            pltpu.VMEM((4, STRIP, HALF_A), F32),
            dma((3,)),
            dma((NA_DEV,)),
            dma((17,)),
            dma((17,)),
            dma((3,)),
            dma((3,)),
            dma((4,)),
            dma((4,)),
            dma((2, 8, 2)),
            dma((2, 8, 2)),
            dma((16,)),
            dma((16,)),
            dma((16,)),
            dma((3, 4)),
            dma((3,)),
            dma((3,)),
            dma((4,)),
            dma((4,)),
        ],
        compiler_params=pltpu.CompilerParams(
            collective_id=0, has_side_effects=True, vmem_limit_bytes=67043328
        ),
    )(eri_tiles, screen.T, density_bra.T, density_ket.T)
    return bra_t.T, ket_t.T


def solution(mesh):
    return jax.shard_map(
        body,
        mesh=mesh,
        in_specs=(
            P("row", ("col", "depth"), None, None),
            P("row", ("col", "depth")),
            P("row", "col"),
            P(("col", "depth"), "row"),
        ),
        out_specs=(P("row", "col"), P(("col", "depth"), "row")),
        check_vma=False,
    )
```

time: 141 us -> 60.5 us (0.43)
  the two profiles are of different devices: /device:TPU:8 before, /device:TPU:2 now
where the time goes in v1:
time: 60.5 us; the launch traced here: 60 us
  Pallas kernels  56.2 us (93%)
  local copies, waits for them, and re-layouts  3.09 us (5%)
  between operations  0.64 us (1%)
    pallas_call x1, Pallas kernels, body(): pl.pallas_call(kernel, out_shape=(jax.ShapeDtypeStruct((32, ROWS_A), F32)...  56.2 us
    unnamed x2, local copies, waits for them, and re-layouts  3.09 us

profile of v1, /device:TPU:2, one launch (start us, length us, event | category | flops | bytes accessed | tf_op | source)
XLA Modules:
  0.0 60.0 jit_solution(2929549523707855514)
XLA Ops:
  0.6 56.2 %shard_map.59 = (f32[32,1536]{1,0:T(8,128)}, f32[16,1024]{1,0:T(8,128)}) custom-call(bf16[12,8,128,128]{3,2,1,0:T(8,128)(2,1)} %eri_hbm.1, s32[8,12]{1,0:T(8,128)} %bitcast.9, bf16[32,1536]{1,0:T(8,128)(2,1)} %bitcast.6, bf16[16,1024]{1,0:T(8,128)(2,1)} %bitcast.8), custom_call_target="tpu_custom_call" | custom-call | tf_op jit(solution)/shard_map/pallas_call | solution.py:355
  56.9 1.6 %copy.8 = f32[1536,32]{0,1:T(8,128)} copy(f32[1536,32]{0,1:T(8,128)} %bitcast.5) | data formatting | bytes 393216
  58.5 1.5 %copy.9 = f32[1024,16]{0,1:T(8,128)} copy(f32[1024,16]{0,1:T(8,128)} %bitcast.7) | data formatting | bytes 131072
